TPU v7x, 256 devices: a whole 4x4x8 slice. The times are simulated.
256 devices in a mesh: tm: 8 (over x_hi, y), rows: 32 (over x_lo, z, core).
Axes of the slice: x: 4 (x_hi: 2, x_lo: 2; x = x_hi * 2 + x_lo), y: 4, z: 8, core: 2. Of those that a mesh axis runs over, the one named last changes fastest.
Arguments:
- record: bfloat16 [2, 65536, 4096], P(None, 'rows', 'tm'), may hold values from -6 to 6
- seed_list: int32 [4], replicated, may hold values from 0 to 65535
- block_offsets: int32 [2], replicated, may hold values from 0 to 1048575
Outputs:
- range_sketch: float32 [65536, 128], P('rows')
- corange_sketch: float32 [2, 256, 4096], P(None, 'rows', 'tm')
- core_sketch: float32 [384, 384], P('rows')
Inputs may be any that keep to these rules, and one draw needn't show every extreme that they name: `seed_list`: entries 0, 1, 2, 3 seed the range, co-range, core row and core column test matrices.
All inputs are finite; a program needn't handle non-finite values.
Results may differ from a plain program's by a relative error of at most 0.0041.
Values sent between devices are 32-bit elements; how exact they have to be, the bound alone decides.
A program may use at most 64 MiB of HBM per device.

v0:
```python
import math
import jax
import jax.numpy as jnp
from jax import lax
from jax.sharding import PartitionSpec as P

RANGE = 128
CORANGE = 256
CORE = 384


def in_blocks(x, dim, size):
    before, after = (x.shape[:dim], x.shape[dim + 1 :])
    return jnp.moveaxis(x.reshape(*before, size, -1, *after), dim, 0)


def sum_at_owner(x, axis, dim):
    parts = in_blocks(x, dim, lax.axis_size(axis))
    arrived = lax.all_to_all(parts, axis, split_axis=0, concat_axis=0, tiled=True)
    return arrived.sum(axis=0)


def from_everyone(x, axis):
    size = lax.axis_size(axis)
    return lax.all_to_all(jnp.broadcast_to(x[None], (size, *x.shape)), axis, 0, 0, tiled=True)


def taken_together(x, axis):
    return from_everyone(x, axis).sum(axis=0)


def shift_down(values, amount):
    return lax.shift_right_logical(values, jnp.full(values.shape, amount, jnp.int32))


def sketch_matrix(seed_value, first_ids, second_ids, factor):
    hashed = (
        first_ids[:, None] * 668265263 + second_ids[None, :] * 374761393 + seed_value * 625341585
    )
    hashed = jnp.bitwise_xor(hashed, shift_down(hashed, 15))
    hashed = hashed * 739982445
    hashed = jnp.bitwise_xor(hashed, shift_down(hashed, 12))
    hashed = hashed * 695872825
    hashed = jnp.bitwise_xor(hashed, shift_down(hashed, 15))
    byte_sum = jnp.bitwise_and(hashed, 255)
    byte_sum = byte_sum + jnp.bitwise_and(shift_down(hashed, 8), 255)
    byte_sum = byte_sum + jnp.bitwise_and(shift_down(hashed, 16), 255)
    byte_sum = byte_sum + jnp.bitwise_and(shift_down(hashed, 24), 255)
    return ((byte_sum - 510).astype(jnp.float32) * factor).astype(jnp.bfloat16)


def sum_range(part):
    return lax.psum(part, "tm")


def sum_corange(parts):
    return sum_at_owner(parts, "rows", 1)


def sum_core(part):
    share = sum_at_owner(part, "rows", 0)
    return taken_together(share, "tm")


def shards(record, seed_list, block_offsets):
    blocks, rows_dev, cols_dev = record.shape
    rows_count = lax.axis_size("rows")
    time_count = lax.axis_size("tm")
    row_factor = 1.0 / (147.8 * math.sqrt(rows_dev * rows_count))
    col_factor = 1.0 / (147.8 * math.sqrt(blocks * cols_dev * time_count))
    row_ids = lax.axis_index("rows") * rows_dev + jnp.arange(rows_dev, dtype=jnp.int32)
    psi_rows = sketch_matrix(
        seed_list[1], jnp.arange(CORANGE, dtype=jnp.int32), row_ids, row_factor
    )
    phi_rows = sketch_matrix(seed_list[2], jnp.arange(CORE, dtype=jnp.int32), row_ids, row_factor)
    col_base = lax.axis_index("tm") * cols_dev + jnp.arange(cols_dev, dtype=jnp.int32)
    range_local = jnp.zeros((rows_dev, RANGE), jnp.float32)
    core_local = jnp.zeros((CORE, CORE), jnp.float32)
    range_sketch = None
    core_sketch = None
    corange_parts = []
    for number in range(blocks):
        matrix = record[number]
        col_ids = block_offsets[number] + col_base
        omega_cols = sketch_matrix(
            seed_list[0], col_ids, jnp.arange(RANGE, dtype=jnp.int32), col_factor
        )
        xi_cols = sketch_matrix(
            seed_list[3], jnp.arange(CORE, dtype=jnp.int32), col_ids, col_factor
        )
        range_part = jnp.dot(matrix, omega_cols, preferred_element_type=jnp.float32)
        corange_part = jnp.dot(psi_rows, matrix, preferred_element_type=jnp.float32)
        projected = jnp.dot(phi_rows, matrix, preferred_element_type=jnp.float32)
        core_part = jnp.dot(
            projected, xi_cols.astype(jnp.float32).T, precision=lax.Precision.HIGHEST
        )
        range_local = range_local + range_part
        core_local = core_local + core_part
        corange_parts.append(corange_part)
    range_sketch = sum_range(range_local)
    core_sketch = sum_core(core_local)
    corange_sketch = sum_corange(jnp.stack(corange_parts))
    return (range_sketch, corange_sketch, core_sketch)


def solution(mesh):
    placed = (P(None, "rows", "tm"), P(), P())
    return jax.shard_map(
        shards,
        mesh=mesh,
        in_specs=placed,
        out_specs=(P("rows", None), P(None, "rows", "tm"), P("rows", None)),
        check_vma=False,
    )
```

profile of v0, /device:TPU:32, one launch (start us, length us, event | category | flops | bytes accessed | tf_op | source)
XLA Modules:
  0.0 185.7 jit_solution(12413052100564470267)
XLA Ops:
  7.2 1.5 fusion.175
  9.3 0.0 copy-start.1
  9.3 4.2 %fusion.9 = f32[384,512]{1,0:T(8,128)S(1)} fusion(bf16[2,2048,512]{2,1,0:T(8,128)(2,1)} %param.3, s32[]{:T(128)} %bitcast.12, s32[2048]{0:T(1024)S(1)} %add_multiply_fusion.1, s32[384]{0:T(512)S(1)} %iota_multiply_fusion), kind=kOutput, calls=%fused_computation.17 | convolution fusion | flops 824180736 | bytes 2893824 | tf_op jit(solution)/shard_map/dot_general | solution.py:93
  13.5 0.0 copy-done.1
  13.5 0.0 copy-start
  13.5 2.5 %fusion.12 = f32[384,512]{1,0:T(8,128)S(1)} fusion(bf16[2,2048,512]{2,1,0:T(8,128)(2,1)S(1)} %copy-done.1, s32[]{:T(128)} %bitcast.12, s32[2048]{0:T(1024)S(1)} %add_multiply_fusion.1, s32[384]{0:T(512)S(1)} %iota_multiply_fusion), kind=kOutput, calls=%fused_computation.20 | convolution fusion | flops 824180736 | bytes 2893828 | tf_op jit(solution)/shard_map/dot_general | solution.py:93
  16.0 0.0 copy-done
  16.0 0.6 fusion.176
  17.3 1.3 fusion.91
  18.6 1.4 fusion.32
  20.0 1.4 convolution_add_fusion.1
  21.3 0.9 reshape.121
  22.3 9.7 %all-to-all-start.1 = ((f32[32,12,384]{2,1,0:T(8,128)}), f32[32,12,384]{2,1,0:T(8,128)S(1)}, u32[]{:S(2)}, u32[]{:S(2)}) async-start(f32[32,12,384]{2,1,0:T(8,128)} %reshape.121), calls=%async_computation.1 | async-start | bytes 1572864 | tf_op jit(solution)/shard_map/all_to_all | solution.py:19
  32.6 0.0 copy-start.2
  32.6 3.4 %fusion.25 = f32[1,32,8,512]{3,2,1,0:T(8,128)S(1)} fusion(bf16[2,2048,512]{2,1,0:T(8,128)(2,1)} %param.3, s32[]{:T(128)} %bitcast.6, s32[2048]{0:T(1024)S(1)} %add_multiply_fusion.1, s32[32,8]{1,0:T(8,128)S(1)} %add_multiply_fusion), kind=kOutput, calls=%fused_computation.33 | convolution fusion | flops 549453824 | bytes 2631168 | tf_op jit(solution)/shard_map/dot_general | solution.py:92
  36.0 0.0 copy-done.2
  36.0 1.7 fusion.22
  37.7 17.6 %all-to-all-done.1 = f32[32,12,384]{2,1,0:T(8,128)S(1)} async-done(((f32[32,12,384]{2,1,0:T(8,128)}), f32[32,12,384]{2,1,0:T(8,128)S(1)}, u32[]{:S(2)}, u32[]{:S(2)}) %all-to-all-start.1) | async-done | bytes 589856 | tf_op jit(solution)/shard_map/all_to_all | solution.py:19
  55.3 0.1 reduce_sum.28
  55.4 0.7 broadcast_in_dim.50
  56.0 6.6 %all-to-all-start.2 = ((f32[8,12,384]{2,1,0:T(8,128)}), f32[8,12,384]{2,1,0:T(8,128)S(1)}, u32[]{:S(2)}, u32[]{:S(2)}) async-start(f32[8,12,384]{2,1,0:T(8,128)} %broadcast_in_dim.50), calls=%async_computation.2 | async-start | bytes 393216 | tf_op jit(solution)/shard_map/all_to_all | solution.py:25
  62.7 0.1 maximum_bitcast_fusion
  62.8 1.1 copy.12
  63.8 7.3 %all-to-all-done.2 = f32[8,12,384]{2,1,0:T(8,128)S(1)} async-done(((f32[8,12,384]{2,1,0:T(8,128)}), f32[8,12,384]{2,1,0:T(8,128)S(1)}, u32[]{:S(2)}, u32[]{:S(2)}) %all-to-all-start.2) | async-done | bytes 147488 | tf_op jit(solution)/shard_map/all_to_all | solution.py:25
  71.1 3.8 %all-to-all-start = ((f32[32,2,8,512]{3,2,1,0:T(8,128)}), f32[32,2,8,512]{3,2,1,0:T(8,128)S(1)}, u32[]{:S(2)}, u32[]{:S(2)}) async-start(f32[32,2,8,512]{3,2,1,0:T(8,128)} %copy.12), calls=%async_computation | async-start | bytes 2097152 | tf_op jit(solution)/shard_map/all_to_all | solution.py:19
  74.9 0.0 all-reduce.2.cloned.1.call-start
  75.6 1.3 fusion.92
  76.9 2.6 %fusion.14 = f32[128,2048]{1,0:T(8,128)S(1)} fusion(bf16[2,2048,512]{2,1,0:T(8,128)(2,1)} %param.3, s32[]{:T(128)} %bitcast.1, s32[128]{0:T(128)S(1)} %iota_multiply_fusion.1, s32[512]{0:T(512)S(1)} %get-tuple-element.26), kind=kOutput, calls=%fused_computation.22 | convolution fusion | flops 270008320 | bytes 3148800 | tf_op jit(solution)/shard_map/dot_general | solution.py:91
  79.5 3.6 %fusion.2 = f32[2048,128]{0,1:T(8,128)} fusion(f32[128,2048]{1,0:T(8,128)S(1)} %fusion.14, bf16[2,2048,512]{2,1,0:T(8,128)(2,1)} %param.3, s32[512]{0:T(512)S(1)} %get-tuple-element.27, s32[]{:T(128)} %bitcast.1, s32[128]{0:T(128)S(1)} %iota_multiply_fusion.1), kind=kOutput, calls=%fused_computation.10 | convolution fusion | flops 270270464 | bytes 4197376 | tf_op jit(solution)/shard_map/dot_general | solution.py:91
  83.1 0.0 all-reduce.2.cloned.1.call-update
  83.2 91.9 %all-reduce.2.cloned.1.call-done = f32[2048,128]{0,1:T(8,128)} async-done(((f32[2048,128]{0,1:T(8,128)}), f32[2048,128]{0,1:T(8,128)}) %all-reduce.2.cloned.1.call-update) | async-done | bytes 1048592 | tf_op jit(solution)/shard_map/psum | solution.py:53
  175.0 2.5 %copy.14 = f32[2048,128]{1,0:T(8,128)} copy(f32[2048,128]{0,1:T(8,128)} %all-reduce.2.cloned.1.call-done) | data formatting | bytes 2097152
  177.6 0.6 reduce_sum.29
  178.2 0.0 all-to-all-done
  178.2 0.7 reduce_sum.27
  (4 shorter events, 0.0 us)
Async XLA Ops:
  9.3 4.2 %copy-start.1 = (bf16[2,2048,512]{2,1,0:T(8,128)(2,1)S(1)}, bf16[2,2048,512]{2,1,0:T(8,128)(2,1)}, u32[]{:S(2)}) copy-start(bf16[2,2048,512]{2,1,0:T(8,128)(2,1)} %param.3) | copy-start | bytes 12582916
  13.5 2.5 %copy-start = (s32[2]{0:T(128)S(1)}, s32[2]{0:T(128)}, u32[]{:S(2)}) copy-start(s32[2]{0:T(128)} %param.5) | copy-start | bytes 28
  22.3 33.0 %all-to-all-start.1 = ((f32[32,12,384]{2,1,0:T(8,128)}), f32[32,12,384]{2,1,0:T(8,128)S(1)}, u32[]{:S(2)}, u32[]{:S(2)}) async-start(f32[32,12,384]{2,1,0:T(8,128)} %reshape.121), calls=%async_computation.1 | async-start | bytes 1572864 | tf_op jit(solution)/shard_map/all_to_all | solution.py:19
  32.6 3.4 %copy-start.2 = (bf16[2,2048,512]{2,1,0:T(8,128)(2,1)S(1)}, bf16[2,2048,512]{2,1,0:T(8,128)(2,1)}, u32[]{:S(2)}) copy-start(bf16[2,2048,512]{2,1,0:T(8,128)(2,1)} %param.3) | copy-start | bytes 12582916
  56.0 15.1 %all-to-all-start.2 = ((f32[8,12,384]{2,1,0:T(8,128)}), f32[8,12,384]{2,1,0:T(8,128)S(1)}, u32[]{:S(2)}, u32[]{:S(2)}) async-start(f32[8,12,384]{2,1,0:T(8,128)} %broadcast_in_dim.50), calls=%async_computation.2 | async-start | bytes 393216 | tf_op jit(solution)/shard_map/all_to_all | solution.py:25
  71.1 107.1 %all-to-all-start = ((f32[32,2,8,512]{3,2,1,0:T(8,128)}), f32[32,2,8,512]{3,2,1,0:T(8,128)S(1)}, u32[]{:S(2)}, u32[]{:S(2)}) async-start(f32[32,2,8,512]{3,2,1,0:T(8,128)} %copy.12), calls=%async_computation | async-start | bytes 2097152 | tf_op jit(solution)/shard_map/all_to_all | solution.py:19
  74.9 100.1 %all-reduce.2.cloned.1.call-start = ((), (), s32[]{:S(2)}) async-start(), calls=%async_computation.3 | async-start | bytes 2097152 | tf_op jit(solution)/shard_map/psum | solution.py:53
Sparse Core Ops, SparseCore 0:
  83.3 91.7 all-reduce.1
where the time goes:
time: 186 us
  waiting for transfers between devices  117 us (63%)
  matrix products  20.8 us (11%)
  starting transfers between devices  20.1 us (11%)
  between operations  16.8 us (9%)
  local copies, waits for them, and re-layouts  7.35 us (4%)
  other arithmetic  3.97 us (2%)
    psum x1, waiting for transfers between devices, sum_range(): return lax.psum(part, 'tm')  91.9 us
    all_to_all x2, waiting for transfers between devices, sum_at_owner(): lax.all_to_all(parts, axis, split_axis=0, concat_axis=0, tiled=True)  17.6 us
    all_to_all x2, starting transfers between devices, sum_at_owner(): lax.all_to_all(parts, axis, split_axis=0, concat_axis=0, tiled=True)  13.4 us
    all_to_all x1, waiting for transfers between devices, from_everyone(): lax.all_to_all(jnp.broadcast_to(x[None], (size, *x.shape)), axis, 0, 0, t...  7.3 us
    dot_general x2, matrix products, shards(): projected = jnp.dot(phi_rows, matrix, preferred_element_type=jnp.float32)  6.71 us
    all_to_all x1, starting transfers between devices, from_everyone(): lax.all_to_all(jnp.broadcast_to(x[None], (size, *x.shape)), axis, 0, 0, t...  6.64 us
    dot_general x2, matrix products, shards(): range_part = jnp.dot(matrix, omega_cols, preferred_element_type=jnp.float32)  6.24 us
    dot_general x2, matrix products, shards(): corange_part = jnp.dot(psi_rows, matrix, preferred_element_type=jnp.float32)  5.1 us
  transfers between devices with their start and end apart: 4, of which 3 were waited for; matrix products, arithmetic and copies ran while one was open for 9% of the time, Pallas kernels for 0%

commit v1 on v0

--- a/solution.py
+++ b/solution.py
@@ -50,7 +50,7 @@
 
 
 def sum_range(part):
-    return lax.psum(part, "tm")
+    return jnp.sum(lax.all_gather(part, "tm"), axis=0)
 
 
 def sum_corange(parts):

time: 186 us -> 171 us (0.919)
  waiting for transfers between devices: 117 us -> 89.3 us
  local copies, waits for them, and re-layouts: 7.35 us -> 17.6 us
  other arithmetic: 3.97 us -> 6.17 us
    psum x1 -> x0, waiting for transfers between devices: 91.9 us -> none  [sum_range(): return lax.psum(part, 'tm')]
    all_gather x0 -> x1, waiting for transfers between devices: none -> 35.2 us  [sum_range(): return jnp.sum(lax.all_gather(part, 'tm'), axis=0)]
    all_to_all x2, waiting for transfers between devices: 17.6 us -> 45.7 us  [sum_at_owner(): lax.all_to_all(parts, axis, split_axis=0, concat_axis=0, tiled=True)]
    unnamed x7 -> x6, local copies, waits for them, and re-layouts: 2.55 us -> 12 us
    reduce_sum x0 -> x1, other arithmetic: none -> 2.1 us  [sum_range(): return jnp.sum(lax.all_gather(part, 'tm'), axis=0)]
  transfers between devices with their start and end apart: 4 -> 4, of which waited for: 3 -> 4; matrix products, arithmetic and copies ran while one was open for 9% -> 12% of each run, Pallas kernels for 0% -> 0%
where the time goes in v1:
time: 171 us; the launch traced here: 170 us
  waiting for transfers between devices  89.3 us (52%)
  matrix products  20.6 us (12%)
  starting transfers between devices  20.1 us (12%)
  local copies, waits for them, and re-layouts  17.6 us (10%)
  between operations  16.6 us (10%)
  other arithmetic  6.17 us (4%)
    all_to_all x2, waiting for transfers between devices, sum_at_owner(): lax.all_to_all(parts, axis, split_axis=0, concat_axis=0, tiled=True)  45.7 us
    all_gather x1, waiting for transfers between devices, sum_range(): return jnp.sum(lax.all_gather(part, 'tm'), axis=0)  35.2 us
    all_to_all x2, starting transfers between devices, sum_at_owner(): lax.all_to_all(parts, axis, split_axis=0, concat_axis=0, tiled=True)  13.4 us
    unnamed x6, local copies, waits for them, and re-layouts  12 us
    all_to_all x1, waiting for transfers between devices, from_everyone(): lax.all_to_all(jnp.broadcast_to(x[None], (size, *x.shape)), axis, 0, 0, t...  8.37 us
    all_to_all x1, starting transfers between devices, from_everyone(): lax.all_to_all(jnp.broadcast_to(x[None], (size, *x.shape)), axis, 0, 0, t...  6.64 us
    dot_general x2, matrix products, shards(): projected = jnp.dot(phi_rows, matrix, preferred_element_type=jnp.float32)  6.56 us
    dot_general x2, matrix products, shards(): range_part = jnp.dot(matrix, omega_cols, preferred_element_type=jnp.float32)  6.21 us
  transfers between devices with their start and end apart: 4, of which 4 were waited for; matrix products, arithmetic and copies ran while one was open for 12% of the time, Pallas kernels for 0%

profile of v1, /device:TPU:32, one launch (start us, length us, event | category | flops | bytes accessed | tf_op | source)
XLA Modules:
  0.0 170.4 jit_solution(11775754372544489531)
XLA Ops:
  7.2 0.0 all-gather.3.cloned.1.call-start
  7.2 1.4 fusion.175
  8.6 1.4 fusion.176
  10.7 1.3 fusion.92
  12.0 2.6 %fusion.14 = f32[128,2048]{1,0:T(8,128)S(1)} fusion(bf16[2,2048,512]{2,1,0:T(8,128)(2,1)} %param.3, s32[]{:T(128)} %bitcast.1, s32[128]{0:T(128)S(1)} %iota_multiply_fusion.1, s32[512]{0:T(512)S(1)} %get-tuple-element.20), kind=kOutput, calls=%fused_computation.23 | convolution fusion | flops 270008320 | bytes 3148800 | tf_op jit(solution)/shard_map/dot_general | solution.py:91
  14.6 3.6 %fusion.2 = f32[2048,128]{0,1:T(8,128)} fusion(f32[128,2048]{1,0:T(8,128)S(1)} %fusion.14, bf16[2,2048,512]{2,1,0:T(8,128)(2,1)} %param.3, s32[512]{0:T(512)S(1)} %get-tuple-element.21, s32[]{:T(128)} %bitcast.1, s32[128]{0:T(128)S(1)} %iota_multiply_fusion.1), kind=kOutput, calls=%fused_computation.11 | convolution fusion | flops 270270464 | bytes 4197376 | tf_op jit(solution)/shard_map/dot_general | solution.py:91
  18.2 0.0 all-gather.3.cloned.1.call-update
  19.4 1.3 fusion.91
  20.7 4.1 %fusion.12 = f32[384,512]{1,0:T(8,128)S(1)} fusion(bf16[2,2048,512]{2,1,0:T(8,128)(2,1)} %param.3, s32[]{:T(128)} %bitcast.12, s32[2048]{0:T(1024)S(1)} %add_multiply_fusion.1, s32[384]{0:T(512)S(1)} %iota_multiply_fusion), kind=kOutput, calls=%fused_computation.21 | convolution fusion | flops 824180736 | bytes 2893824 | tf_op jit(solution)/shard_map/dot_general | solution.py:93
  24.8 0.0 copy-start
  24.8 1.3 fusion.32
  26.2 0.8 copy-done
  27.0 2.5 %fusion.9 = f32[384,512]{1,0:T(8,128)S(1)} fusion(bf16[2,2048,512]{2,1,0:T(8,128)(2,1)S(1)} %copy-done, s32[]{:T(128)} %bitcast.12, s32[2048]{0:T(1024)S(1)} %add_multiply_fusion.1, s32[384]{0:T(512)S(1)} %iota_multiply_fusion), kind=kOutput, calls=%fused_computation.18 | convolution fusion | flops 824180736 | bytes 2893828 | tf_op jit(solution)/shard_map/dot_general | solution.py:93
  29.5 1.4 convolution_add_fusion.1
  30.8 1.0 reshape.121
  31.8 9.7 %all-to-all-start.1 = ((f32[32,12,384]{2,1,0:T(8,128)}), f32[32,12,384]{2,1,0:T(8,128)S(1)}, u32[]{:S(2)}, u32[]{:S(2)}) async-start(f32[32,12,384]{2,1,0:T(8,128)} %reshape.121), calls=%async_computation.1 | async-start | bytes 1572864 | tf_op jit(solution)/shard_map/all_to_all | solution.py:19
  42.2 0.0 copy-start.1
  42.2 3.4 %fusion.25 = f32[1,32,8,512]{3,2,1,0:T(8,128)S(1)} fusion(bf16[2,2048,512]{2,1,0:T(8,128)(2,1)} %param.3, s32[]{:T(128)} %bitcast.6, s32[2048]{0:T(1024)S(1)} %add_multiply_fusion.1, s32[32,8]{1,0:T(8,128)S(1)} %add_multiply_fusion), kind=kOutput, calls=%fused_computation.34 | convolution fusion | flops 549453824 | bytes 2631168 | tf_op jit(solution)/shard_map/dot_general | solution.py:92
  45.6 0.0 copy-done.1
  45.6 1.7 fusion.22
  47.3 17.6 %all-to-all-done.1 = f32[32,12,384]{2,1,0:T(8,128)S(1)} async-done(((f32[32,12,384]{2,1,0:T(8,128)}), f32[32,12,384]{2,1,0:T(8,128)S(1)}, u32[]{:S(2)}, u32[]{:S(2)}) %all-to-all-start.1) | async-done | bytes 589856 | tf_op jit(solution)/shard_map/all_to_all | solution.py:19
  64.9 0.1 reduce_sum.38
  64.9 0.7 broadcast_in_dim.50
  65.6 6.6 %all-to-all-start.2 = ((f32[8,12,384]{2,1,0:T(8,128)}), f32[8,12,384]{2,1,0:T(8,128)S(1)}, u32[]{:S(2)}, u32[]{:S(2)}) async-start(f32[8,12,384]{2,1,0:T(8,128)} %broadcast_in_dim.50), calls=%async_computation.2 | async-start | bytes 393216 | tf_op jit(solution)/shard_map/all_to_all | solution.py:25
  72.2 0.1 maximum_bitcast_fusion
  72.3 1.1 copy.10
  73.5 8.4 %all-to-all-done.2 = f32[8,12,384]{2,1,0:T(8,128)S(1)} async-done(((f32[8,12,384]{2,1,0:T(8,128)}), f32[8,12,384]{2,1,0:T(8,128)S(1)}, u32[]{:S(2)}, u32[]{:S(2)}) %all-to-all-start.2) | async-done | bytes 147488 | tf_op jit(solution)/shard_map/all_to_all | solution.py:25
  81.8 3.7 %all-to-all-start = ((f32[32,2,8,512]{3,2,1,0:T(8,128)}), f32[32,2,8,512]{3,2,1,0:T(8,128)S(1)}, u32[]{:S(2)}, u32[]{:S(2)}) async-start(f32[32,2,8,512]{3,2,1,0:T(8,128)} %copy.10), calls=%async_computation | async-start | bytes 2097152 | tf_op jit(solution)/shard_map/all_to_all | solution.py:19
  85.6 0.6 reduce_sum.39
  86.2 28.2 %all-to-all-done = f32[32,2,8,512]{3,2,1,0:T(8,128)S(1)} async-done(((f32[32,2,8,512]{3,2,1,0:T(8,128)}), f32[32,2,8,512]{3,2,1,0:T(8,128)S(1)}, u32[]{:S(2)}, u32[]{:S(2)}) %all-to-all-start) | async-done | bytes 1048608 | tf_op jit(solution)/shard_map/all_to_all | solution.py:19
  114.4 0.7 reduce_sum.37
  115.1 35.2 %all-gather.3.cloned.1.call-done = f32[16384,128]{0,1:T(8,128)} async-done(((f32[2048,128]{0,1:T(8,128)}), f32[16384,128]{0,1:T(8,128)}) %all-gather.3.cloned.1.call-update) | async-done | bytes 8388624 | tf_op jit(solution)/shard_map/all_gather | solution.py:53
  150.3 9.9 %copy.14 = f32[16,8,8,2048]{3,2,1,0:T(8,128)S(1)} copy(f32[16,8,8,2048]{3,1,2,0:T(8,128)} %bitcast.41) | data formatting | bytes 16777216
  160.1 2.1 %bitcast_reduce_fusion = f32[2048,128]{0,1:T(8,128)S(1)} fusion(f32[16,8,8,2048]{3,2,1,0:T(8,128)S(1)} %copy.14), kind=kLoop, calls=%fused_computation | loop fusion | flops 1835008 | bytes 9437184 | tf_op jit(solution)/shard_map/reduce_sum | solution.py:53
  162.2 1.3 copy.12
  (4 shorter events, 0.0 us)
Async XLA Ops:
  7.2 143.1 %all-gather.3.cloned.1.call-start = ((), (), s32[]{:S(2)}) async-start(), calls=%async_computation.3 | async-start | bytes 9437184 | tf_op jit(solution)/shard_map/all_gather | solution.py:53
  24.8 2.2 %copy-start = (bf16[2,2048,512]{2,1,0:T(8,128)(2,1)S(1)}, bf16[2,2048,512]{2,1,0:T(8,128)(2,1)}, u32[]{:S(2)}) copy-start(bf16[2,2048,512]{2,1,0:T(8,128)(2,1)} %param.3) | copy-start | bytes 12582916
  31.8 33.0 %all-to-all-start.1 = ((f32[32,12,384]{2,1,0:T(8,128)}), f32[32,12,384]{2,1,0:T(8,128)S(1)}, u32[]{:S(2)}, u32[]{:S(2)}) async-start(f32[32,12,384]{2,1,0:T(8,128)} %reshape.121), calls=%async_computation.1 | async-start | bytes 1572864 | tf_op jit(solution)/shard_map/all_to_all | solution.py:19
  42.2 3.4 %copy-start.1 = (bf16[2,2048,512]{2,1,0:T(8,128)(2,1)S(1)}, bf16[2,2048,512]{2,1,0:T(8,128)(2,1)}, u32[]{:S(2)}) copy-start(bf16[2,2048,512]{2,1,0:T(8,128)(2,1)} %param.3) | copy-start | bytes 12582916
  65.6 16.2 %all-to-all-start.2 = ((f32[8,12,384]{2,1,0:T(8,128)}), f32[8,12,384]{2,1,0:T(8,128)S(1)}, u32[]{:S(2)}, u32[]{:S(2)}) async-start(f32[8,12,384]{2,1,0:T(8,128)} %broadcast_in_dim.50), calls=%async_computation.2 | async-start | bytes 393216 | tf_op jit(solution)/shard_map/all_to_all | solution.py:25
  81.8 32.5 %all-to-all-start = ((f32[32,2,8,512]{3,2,1,0:T(8,128)}), f32[32,2,8,512]{3,2,1,0:T(8,128)S(1)}, u32[]{:S(2)}, u32[]{:S(2)}) async-start(f32[32,2,8,512]{3,2,1,0:T(8,128)} %copy.10), calls=%async_computation | async-start | bytes 2097152 | tf_op jit(solution)/shard_map/all_to_all | solution.py:19
Sparse Core Ops, SparseCore 0:
  18.3 131.8 all-gather.2
